TPU v7x, 128 devices: a whole 4x4x4 slice. The times are simulated.
128 devices in a mesh: gx: 4 (over y), gy: 8 (over z, x_hi), gz: 4 (over x_lo, core).
Axes of the slice: x: 4 (x_hi: 2, x_lo: 2; x = x_hi * 2 + x_lo), y: 4, z: 4, core: 2. Of those that a mesh axis runs over, the one named last changes fastest.
Arguments:
- right_side: float32 [64, 1024, 1024], P('gz', 'gx', 'gy'), may hold values from -8 to 8
- diagonal: float32 [64, 1024, 1024], P('gz', 'gx', 'gy'), may hold values from 0.02 to 1
- regime: int32 [1024, 1024], P('gx', 'gy'), may hold values from 0 to 7
- inverses: float32 [8, 64, 64], replicated, as said below
Outputs:
- solution: float32 [64, 1024, 1024], P('gz', 'gx', 'gy')
- residual: float32 [64, 1024, 1024], P('gz', 'gx', 'gy')
Inputs may be any that keep to these rules, and one draw needn't show every extreme that they name: `inverses`: each block is symmetric positive definite.
All inputs are finite; a program needn't handle non-finite values.
Results may differ from a plain program's by a relative error of at most 0.00025.
Values sent between devices are 32-bit elements; how exact they have to be, the bound alone decides.
A program may use at most 128 MiB of HBM per device.

v0:
```python
import jax
import jax.numpy as jnp
from jax import lax
from jax.sharding import Mesh
from jax.sharding import PartitionSpec as P

NREG = 8
ITERS = 3
GX_GZ = ("gx", "gz_0", "gz_1")
GY = ("gy_0", "gy_1")
GZ = ("gz_0", "gz_1")
GX_GY_GZ = ("gx", "gy_0", "gy_1", "gz_0", "gz_1")


def extended(cells, sides, width):
    for axis, dim in sides:
        count = lax.axis_size(axis)
        ends = count - 1
        head = lax.slice_in_dim(cells, 0, width, axis=dim)
        tail = lax.slice_in_dim(cells, cells.shape[dim] - width, cells.shape[dim], axis=dim)
        cells = jnp.concatenate(
            [
                lax.ppermute(tail, axis, [(i, (i + 1) % count) for i in range(ends)]),
                cells,
                lax.ppermute(head, axis, [((i + 1) % count, i) for i in range(ends)]),
            ],
            axis=dim,
        )
    return cells


def over_axes(x, axes):
    for axis in axes:
        x = lax.psum(x, axis)
    return x


def sent_together(arrays, axis, split_dim, concat_dim, along):
    ends, at = ([], 0)
    for a in arrays[:-1]:
        at += a.shape[along]
        ends.append(at)
    both = jnp.concatenate(arrays, axis=along)
    return tuple(
        jnp.split(
            lax.all_to_all(both, axis, split_axis=split_dim, concat_axis=concat_dim, tiled=True),
            ends,
            axis=along,
        )
    )


def stencil(padded, grid_field, diagonal):
    beside = padded[2:, 1:-1, 1:-1] + padded[:-2, 1:-1, 1:-1]
    beside = beside + padded[1:-1, 2:, 1:-1] + padded[1:-1, :-2, 1:-1]
    beside = beside + padded[1:-1, 1:-1, 2:] + padded[1:-1, 1:-1, :-2]
    return (6.0 + diagonal) * grid_field - beside


def operate(grid_field, diagonal):
    flat_pad = extended(grid_field, ((GX_GZ, 1), (GY, 2)), 1)
    padded = jnp.pad(flat_pad, ((1, 1), (0, 0), (0, 0)))
    return stencil(padded, grid_field, diagonal)


def apply_blocks(matrices, flattened, chosen):
    result = jnp.zeros((matrices.shape[1], flattened.shape[1]), jnp.float32)
    for member in range(NREG):
        product = jnp.dot(matrices[member], flattened, precision=lax.Precision.HIGHEST)
        result = result + jnp.where(chosen[None, :] == member, product, jnp.zeros_like(product))
    return result


def precondition(grid_field, regime, inverses):
    layers = grid_field.shape[0]
    share_rows = grid_field.shape[1]
    offset = lax.axis_index(GZ) * share_rows
    chosen = lax.dynamic_slice_in_dim(regime, offset, share_rows, 0).reshape(-1)
    result = apply_blocks(inverses, grid_field.reshape(layers, -1), chosen)
    return result.reshape(grid_field.shape)


def paired(residual, precond, image):
    return (
        over_axes(jnp.sum(residual * precond), GX_GY_GZ),
        over_axes(jnp.sum(image * precond), GX_GY_GZ),
    )


def per_device(right_side, diagonal, regime, inverses):
    right_side, diagonal = (
        lax.all_to_all(right_side, GZ, split_axis=1, concat_axis=0, tiled=True),
        lax.all_to_all(diagonal, GZ, split_axis=1, concat_axis=0, tiled=True),
    )
    solution = jnp.zeros_like(right_side)
    residual = right_side
    precond = precondition(residual, regime, inverses)
    image = operate(precond, diagonal)
    inner_rz, inner_wz = paired(residual, precond, image)
    step_len = inner_rz / inner_wz
    search = precond
    along = image
    for iteration in range(ITERS):
        solution = solution + step_len * search
        residual = residual - step_len * along
        if iteration + 1 < ITERS:
            precond = precondition(residual, regime, inverses)
            image = operate(precond, diagonal)
            rz_next, inner_wz = paired(residual, precond, image)
            scaling = rz_next / inner_rz
            step_len = rz_next / (inner_wz - scaling * rz_next / step_len)
            search = precond + scaling * search
            along = image + scaling * along
            inner_rz = rz_next
    solution, residual = sent_together((solution, residual), GZ, 0, 1, 2)
    return (solution, residual)


def solution(mesh):
    split = Mesh(
        mesh.devices.reshape(mesh.shape["gx"], 4, 2, 2, 2), ("gx", "gy_0", "gy_1", "gz_0", "gz_1")
    )
    in_specs = (P(GZ, "gx", GY), P(GZ, "gx", GY), P("gx", GY), P())
    out_specs = (P(GZ, "gx", GY), P(GZ, "gx", GY))
    return jax.shard_map(
        per_device, mesh=split, in_specs=in_specs, out_specs=out_specs, check_vma=False
    )
```

profile of v0, /device:TPU:1, one launch (start us, length us, event | category | flops | bytes accessed | tf_op | source)
XLA Modules:
  0.0 442.0 jit_solution(1391907388788264232)
XLA Ops:
  14.6 19.8 %all-to-all-done = f32[16,256,128]{2,0,1:T(8,128)S(1)} async-done(((f32[16,256,128]{2,0,1:T(8,128)}), f32[16,256,128]{2,0,1:T(8,128)S(1)}, u32[]{:S(2)}, u32[]{:S(2)}) %all-to-all-start) | async-done | bytes 2097184 | tf_op jit(solution)/shard_map/all_to_all | solution.py:92
  34.4 5.9 %all-to-all-start.1 = ((f32[16,256,128]{2,0,1:T(8,128)}), f32[16,256,128]{2,0,1:T(8,128)}, u32[]{:S(2)}, u32[]{:S(2)}) async-start(f32[16,256,128]{2,0,1:T(8,128)} %copy.127), calls=%async_computation.1 | async-start | bytes 4194304 | tf_op jit(solution)/shard_map/all_to_all | solution.py:93
  100.0 5.4 %select_maximum_fusion.8 = f32[66,66,130]{2,1,0:T(8,128)S(1)} fusion(f32[64,66,1]{2,1,0:T(8,128)} %copy.136, f32[64,66,1]{2,1,0:T(8,128)} %copy.135, f32[64,1,128]{2,1,0:T(1,128)S(1)} %bitcast.246, f32[64,64,128]{2,1,0:T(8,128)S(1)} %bitcast.230, f32[64,1,128]{2,1,0:T(1,128)S(1)} %bitcast.249), kind=kLoop, calls=%fused_computation.55 | loop fusion | flops 6795360 | bytes 4461600 | tf_op jit(solution)/shard_map/concatenate | solution.py:21
  105.5 5.7 %multiply_reduce_fusion.4 = (f32[]{:T(128)}, f32[64,64,128]{2,1,0:T(8,128)}) fusion(f32[8,8,64,128]{3,2,1,0:T(8,128)S(1)} %copy.167, f32[64,1,128]{2,1,0:T(1,128)S(1)} %bitcast.247, f32[64,64,128]{2,1,0:T(8,128)S(1)} %bitcast.231, f32[64,1,128]{2,1,0:T(1,128)S(1)} %bitcast.250, f32[64,66,1]{2,1,0:T(8,128)S(1)} %copy-done.15, ...), kind=kLoop, calls=%fused_computation.144 | loop fusion | flops 8912895 | bytes 12682244 | tf_op jit(solution)/shard_map/reduce_sum | solution.py:86
  111.2 9.4 %all-reduce.8 = (f32[]{:T(128)}, f32[]{:T(128)}) all-reduce(f32[]{:T(128)} %fusion.38, f32[]{:T(128)} %get-tuple-element.38), channel_id=1, replica_groups=mesh['gx'=4,'gy_0'=4,'gy_1'=2,'gz_0'=2,'gz_1'=2] {'gx'}, use_global_device_ids=true, to_apply=%region_1.2 | all-reduce | flops 2 | bytes 16 | tf_op jit(solution)/shard_map/psum | solution.py:34
  120.6 12.2 %all-reduce.5 = (f32[]{:T(128)}, f32[]{:T(128)}) all-reduce(f32[]{:T(128)} %get-tuple-element.16, f32[]{:T(128)} %get-tuple-element.17), channel_id=1, replica_groups=mesh['gx'=4,'gy_0'=4,'gy_1'=2,'gz_0'=2,'gz_1'=2] {'gy_0'}, use_global_device_ids=true, to_apply=%region_2.3 | all-reduce | flops 2 | bytes 16 | tf_op jit(solution)/shard_map/psum | solution.py:34
  132.7 6.0 %all-reduce.17 = (f32[]{:T(128)}, f32[]{:T(128)}) all-reduce(f32[]{:T(128)} %get-tuple-element.10, f32[]{:T(128)} %get-tuple-element.11), channel_id=1, replica_groups=mesh['gx'=4,'gy_0'=4,'gy_1'=2,'gz_0'=2,'gz_1'=2] {'gy_1'}, use_global_device_ids=true, to_apply=%region_3.4 | all-reduce | flops 2 | bytes 16 | tf_op jit(solution)/shard_map/psum | solution.py:34
  143.2 11.4 %all-reduce.11 = (f32[]{:T(128)}, f32[]{:T(128)}) all-reduce(f32[]{:T(128)} %get-tuple-element.28, f32[]{:T(128)} %get-tuple-element.29), channel_id=1, replica_groups=mesh['gx'=4,'gy_0'=4,'gy_1'=2,'gz_0'=2,'gz_1'=2] {'gz_1'}, use_global_device_ids=true, to_apply=%region_5.6 | all-reduce | flops 2 | bytes 16 | tf_op jit(solution)/shard_map/psum | solution.py:34
  202.6 5.5 %collective-permute-start.6 = (f32[64,66,1]{1,0,2:T(8,128)S(1)}, f32[64,66,1]{1,0,2:T(8,128)S(1)}, u32[]{:S(2)}, u32[]{:S(2)}) collective-permute-start(f32[64,66,1]{1,0,2:T(8,128)S(1)} %copy.145), channel_id=1, source_target_pairs={{0,4},{4,8},{8,12},{12,16},{16,20},{20,24},{24,28},{1,5},{5,9},{9,... | collective-permute-start | bytes 50696 | tf_op jit(solution)/shard_map/ppermute | solution.py:23
  212.7 6.2 %select_maximum_fusion.4 = f32[66,66,130]{2,1,0:T(8,128)S(1)} fusion(f32[64,66,1]{2,1,0:T(8,128)} %copy.148, f32[64,66,1]{2,1,0:T(8,128)} %copy.147, f32[64,1,128]{2,1,0:T(1,128)S(1)} %bitcast.255, f32[64,64,128]{2,1,0:T(8,128)} %bitcast.234, f32[64,1,128]{2,1,0:T(1,128)S(1)} %bitcast.261), kind=kLoop, calls=%fused_computation.51 | loop fusion | flops 6795360 | bytes 4461600 | tf_op jit(solution)/shard_map/concatenate | solution.py:21
  218.9 6.0 %multiply_reduce_fusion.2 = (f32[]{:T(128)}, f32[]{:T(128)}, f32[64,64,128]{2,1,0:T(8,128)}) fusion(f32[8,8,64,128]{3,2,1,0:T(8,128)S(1)} %copy-done.4, f32[64,64,128]{2,1,0:T(8,128)S(1)} %bitcast_subtract_fusion, f32[64,1,128]{2,1,0:T(1,128)S(1)} %bitcast.256, f32[64,64,128]{2,1,0:T(8,128)S(1)} %bitcast.235, f32[64,1,128]{2,1,0:T(1,128)S(1)} %bitcast.262, ...), kind=kLoop, calls=%fused_computation.142 | loop fusion | flops 9961470 | bytes 14779400 | tf_op jit(solution)/shard_map/reduce_sum | solution.py:86
  224.9 7.0 %all-reduce.7 = (f32[]{:T(128)}, f32[]{:T(128)}) all-reduce(f32[]{:T(128)} %get-tuple-element.5, f32[]{:T(128)} %get-tuple-element.4), channel_id=1, replica_groups=mesh['gx'=4,'gy_0'=4,'gy_1'=2,'gz_0'=2,'gz_1'=2] {'gx'}, use_global_device_ids=true, to_apply=%region_13.14 | all-reduce | flops 2 | bytes 16 | tf_op jit(solution)/shard_map/psum | solution.py:34
  231.9 9.4 %all-reduce.4 = (f32[]{:T(128)}, f32[]{:T(128)}) all-reduce(f32[]{:T(128)} %get-tuple-element.14, f32[]{:T(128)} %get-tuple-element.15), channel_id=1, replica_groups=mesh['gx'=4,'gy_0'=4,'gy_1'=2,'gz_0'=2,'gz_1'=2] {'gy_0'}, use_global_device_ids=true, to_apply=%region_14.15 | all-reduce | flops 2 | bytes 16 | tf_op jit(solution)/shard_map/psum | solution.py:34
  241.3 6.0 %all-reduce.16 = (f32[]{:T(128)}, f32[]{:T(128)}) all-reduce(f32[]{:T(128)} %get-tuple-element.8, f32[]{:T(128)} %get-tuple-element.9), channel_id=1, replica_groups=mesh['gx'=4,'gy_0'=4,'gy_1'=2,'gz_0'=2,'gz_1'=2] {'gy_1'}, use_global_device_ids=true, to_apply=%region_15.16 | all-reduce | flops 2 | bytes 16 | tf_op jit(solution)/shard_map/psum | solution.py:34
  251.7 13.7 %all-reduce.10 = (f32[]{:T(128)}, f32[]{:T(128)}) all-reduce(f32[]{:T(128)} %get-tuple-element.26, f32[]{:T(128)} %get-tuple-element.27), channel_id=1, replica_groups=mesh['gx'=4,'gy_0'=4,'gy_1'=2,'gz_0'=2,'gz_1'=2] {'gz_1'}, use_global_device_ids=true, to_apply=%region_17.18 | all-reduce | flops 2 | bytes 16 | tf_op jit(solution)/shard_map/psum | solution.py:34
  317.6 5.5 %collective-permute-start.10 = (f32[64,66,1]{1,0,2:T(8,128)S(1)}, f32[64,66,1]{1,0,2:T(8,128)S(1)}, u32[]{:S(2)}, u32[]{:S(2)}) collective-permute-start(f32[64,66,1]{1,0,2:T(8,128)S(1)} %copy.157), channel_id=1, source_target_pairs={{0,4},{4,8},{8,12},{12,16},{16,20},{20,24},{24,28},{1,5},{5,9},{9,... | collective-permute-start | bytes 50696 | tf_op jit(solution)/shard_map/ppermute | solution.py:23
  327.6 6.4 %select_maximum_fusion = f32[66,66,130]{2,1,0:T(8,128)S(1)} fusion(f32[64,66,1]{2,1,0:T(8,128)} %copy.160, f32[64,66,1]{2,1,0:T(8,128)} %copy.159, f32[64,1,128]{2,1,0:T(1,128)S(1)} %bitcast.252, f32[64,64,128]{2,1,0:T(8,128)} %bitcast.238, f32[64,1,128]{2,1,0:T(1,128)S(1)} %bitcast.258), kind=kLoop, calls=%fused_computation.47 | loop fusion | flops 6795360 | bytes 4461600 | tf_op jit(solution)/shard_map/concatenate | solution.py:21
  334.1 6.0 %multiply_reduce_fusion = (f32[]{:T(128)}, f32[]{:T(128)}, f32[64,64,128]{2,1,0:T(8,128)}) fusion(f32[8,8,64,128]{3,2,1,0:T(8,128)S(1)} %copy-done.6, f32[64,64,128]{2,1,0:T(8,128)S(1)} %multiply_subtract_fusion.1, f32[64,1,128]{2,1,0:T(1,128)S(1)} %bitcast.253, f32[64,64,128]{2,1,0:T(8,128)S(1)} %bitcast.239, f32[64,1,128]{2,1,0:T(1,128)S(1)} %bitcast.259, ...), kind=kLoop, calls=%fused_computation.138 | loop fusion | flops 9961470 | bytes 14779400 | tf_op jit(solution)/shard_map/reduce_sum | solution.py:86
  340.1 6.6 %all-reduce.6 = (f32[]{:T(128)}, f32[]{:T(128)}) all-reduce(f32[]{:T(128)} %get-tuple-element.3, f32[]{:T(128)} %get-tuple-element.2), channel_id=1, replica_groups=mesh['gx'=4,'gy_0'=4,'gy_1'=2,'gz_0'=2,'gz_1'=2] {'gx'}, use_global_device_ids=true, to_apply=%region_25.26 | all-reduce | flops 2 | bytes 16 | tf_op jit(solution)/shard_map/psum | solution.py:34
  346.7 7.5 %all-reduce.3 = (f32[]{:T(128)}, f32[]{:T(128)}) all-reduce(f32[]{:T(128)} %get-tuple-element.12, f32[]{:T(128)} %get-tuple-element.13), channel_id=1, replica_groups=mesh['gx'=4,'gy_0'=4,'gy_1'=2,'gz_0'=2,'gz_1'=2] {'gy_0'}, use_global_device_ids=true, to_apply=%region_26.27 | all-reduce | flops 2 | bytes 16 | tf_op jit(solution)/shard_map/psum | solution.py:34
  354.2 5.9 %all-reduce.15 = (f32[]{:T(128)}, f32[]{:T(128)}) all-reduce(f32[]{:T(128)} %get-tuple-element.6, f32[]{:T(128)} %get-tuple-element.7), channel_id=1, replica_groups=mesh['gx'=4,'gy_0'=4,'gy_1'=2,'gz_0'=2,'gz_1'=2] {'gy_1'}, use_global_device_ids=true, to_apply=%region_27.28 | all-reduce | flops 2 | bytes 16 | tf_op jit(solution)/shard_map/psum | solution.py:34
  364.6 13.5 %all-reduce.9 = (f32[]{:T(128)}, f32[]{:T(128)}) all-reduce(f32[]{:T(128)} %get-tuple-element.24, f32[]{:T(128)} %get-tuple-element.25), channel_id=1, replica_groups=mesh['gx'=4,'gy_0'=4,'gy_1'=2,'gz_0'=2,'gz_1'=2] {'gz_1'}, use_global_device_ids=true, to_apply=%region_29.30 | all-reduce | flops 2 | bytes 16 | tf_op jit(solution)/shard_map/psum | solution.py:34
  381.9 6.5 %multiply_subtract_fusion = (f32[64,64,128]{2,1,0:T(8,128)S(1)}, f32[64,64,128]{2,1,0:T(8,128)S(1)}) fusion(f32[64,64,128]{2,1,0:T(8,128)S(1)} %multiply_subtract_fusion.1, f32[64,64,128]{2,1,0:T(8,128)} %get-tuple-element.36, f32[]{:T(128)S(6)} %div.25, f32[]{:T(128)S(6)} %div.27, f32[64,64,128]{2,1,0:T(8,128)} %get-tuple-element.37, ...), kind=kLoop, calls=%fused_computation.136 | loop fusion | flops 7864320 | bytes 18874388 | tf_op jit(solution)/shard_map/sub | solution.py:105
  388.7 50.0 %all_to_all.45 = f32[64,64,256]{2,1,0:T(8,128)S(1)} all-to-all(f32[64,64,256]{2,1,0:T(8,128)S(1)} %pad_maximum_fusion), channel_id=1, replica_groups=mesh['gx'=4,'gy_0'=4,'gy_1'=2,'gz_0'=2,'gz_1'=2] {'gz_0','gz_1'}, dimensions={0} | all-to-all | bytes 8388608 | tf_op jit(solution)/shard_map/all_to_all | solution.py:46
  (125 shorter events, 193.6 us)
Async XLA Ops:
  4.8 29.7 %all-to-all-start = ((f32[16,256,128]{2,0,1:T(8,128)}), f32[16,256,128]{2,0,1:T(8,128)S(1)}, u32[]{:S(2)}, u32[]{:S(2)}) async-start(f32[16,256,128]{2,0,1:T(8,128)} %copy.125), calls=%async_computation | async-start | bytes 4194304 | tf_op jit(solution)/shard_map/all_to_all | solution.py:92
  34.4 38.7 %all-to-all-start.1 = ((f32[16,256,128]{2,0,1:T(8,128)}), f32[16,256,128]{2,0,1:T(8,128)}, u32[]{:S(2)}, u32[]{:S(2)}) async-start(f32[16,256,128]{2,0,1:T(8,128)} %copy.127), calls=%async_computation.1 | async-start | bytes 4194304 | tf_op jit(solution)/shard_map/all_to_all | solution.py:93
  41.0 22.7 %copy-start.1 = (f32[16,4,64,128]{3,2,0,1:T(8,128)}, f32[16,4,64,128]{3,2,0,1:T(8,128)S(1)}, u32[]{:S(2)}) copy-start(f32[16,4,64,128]{3,2,0,1:T(8,128)S(1)} %copy.126) | copy-start | bytes 6291460
  67.5 37.9 %copy-start.2 = (f32[8,8,64,128]{3,2,1,0:T(8,128)}, f32[8,8,64,128]{3,2,1,0:T(8,128)S(1)}, u32[]{:S(2)}) copy-start(f32[8,8,64,128]{3,2,1,0:T(8,128)S(1)} %copy.167) | copy-start | bytes 6291460
  67.6 8.6 %collective-permute-start.1 = (f32[64,1,128]{2,0,1:T(8,128)S(1)}, f32[64,1,128]{2,0,1:T(8,128)S(1)}, u32[]{:S(2)}, u32[]{:S(2)}) collective-permute-start(f32[64,1,128]{2,0,1:T(8,128)S(1)} %bitcast.264), channel_id=1, source_target_pairs={{1,0},{2,1},{3,2},{32,3},{33,32},{34,33},{35,34},{64,35},{65,64},{... | collective-permute-start | bytes 98312 | tf_op jit(solution)/shard_map/ppermute | solution.py:25
  69.6 6.7 %collective-permute-start = (f32[64,1,128]{2,0,1:T(8,128)S(1)}, f32[64,1,128]{2,0,1:T(8,128)S(1)}, u32[]{:S(2)}, u32[]{:S(2)}) collective-permute-start(f32[64,1,128]{2,0,1:T(8,128)S(1)} %bitcast.263), channel_id=1, source_target_pairs={{0,1},{1,2},{2,3},{3,32},{32,33},{33,34},{34,35},{35,64},{64,65},{... | collective-permute-start | bytes 98312 | tf_op jit(solution)/shard_map/ppermute | solution.py:23
  84.3 13.4 %collective-permute-start.2 = (f32[64,66,1]{1,0,2:T(8,128)S(1)}, f32[64,66,1]{1,0,2:T(8,128)S(1)}, u32[]{:S(2)}, u32[]{:S(2)}) collective-permute-start(f32[64,66,1]{1,0,2:T(8,128)S(1)} %copy.133), channel_id=1, source_target_pairs={{0,4},{4,8},{8,12},{12,16},{16,20},{20,24},{24,28},{1,5},{5,9},{9,... | collective-permute-start | bytes 50696 | tf_op jit(solution)/shard_map/ppermute | solution.py:23
  89.1 6.4 %collective-permute-start.3 = (f32[64,66,1]{1,0,2:T(8,128)S(1)}, f32[64,66,1]{1,0,2:T(8,128)S(1)}, u32[]{:S(2)}, u32[]{:S(2)}) collective-permute-start(f32[64,66,1]{1,0,2:T(8,128)S(1)} %copy.134), channel_id=1, source_target_pairs={{4,0},{8,4},{12,8},{16,12},{20,16},{24,20},{28,24},{5,1},{9,5},{13... | collective-permute-start | bytes 50696 | tf_op jit(solution)/shard_map/ppermute | solution.py:25
  158.5 60.4 %copy-start = (f32[64,64,128]{2,1,0:T(8,128)}, f32[64,64,128]{2,1,0:T(8,128)S(1)}, u32[]{:S(2)}) copy-start(f32[64,64,128]{2,1,0:T(8,128)S(1)} %bitcast_subtract_fusion) | copy-start | bytes 6291460
  186.5 6.6 %copy-start.3 = (f32[8,8,64,128]{3,2,1,0:T(8,128)}, f32[8,8,64,128]{3,2,1,0:T(8,128)S(1)}, u32[]{:S(2)}) copy-start(f32[8,8,64,128]{3,2,1,0:T(8,128)S(1)} %copy.170) | copy-start | bytes 6291460
  186.6 5.6 %collective-permute-start.5 = (f32[64,1,128]{2,0,1:T(8,128)S(1)}, f32[64,1,128]{2,0,1:T(8,128)S(1)}, u32[]{:S(2)}, u32[]{:S(2)}) collective-permute-start(f32[64,1,128]{2,0,1:T(8,128)S(1)} %bitcast.267), channel_id=1, source_target_pairs={{1,0},{2,1},{3,2},{32,3},{33,32},{34,33},{35,34},{64,35},{65,64},{... | collective-permute-start | bytes 98312 | tf_op jit(solution)/shard_map/ppermute | solution.py:25
  188.9 4.3 collective-permute-start.4
  198.9 9.3 %collective-permute-start.7 = (f32[64,66,1]{1,0,2:T(8,128)S(1)}, f32[64,66,1]{1,0,2:T(8,128)S(1)}, u32[]{:S(2)}, u32[]{:S(2)}) collective-permute-start(f32[64,66,1]{1,0,2:T(8,128)S(1)} %copy.146), channel_id=1, source_target_pairs={{4,0},{8,4},{12,8},{16,12},{20,16},{24,20},{28,24},{5,1},{9,5},{13... | collective-permute-start | bytes 50696 | tf_op jit(solution)/shard_map/ppermute | solution.py:25
  202.6 7.8 %collective-permute-start.6 = (f32[64,66,1]{1,0,2:T(8,128)S(1)}, f32[64,66,1]{1,0,2:T(8,128)S(1)}, u32[]{:S(2)}, u32[]{:S(2)}) collective-permute-start(f32[64,66,1]{1,0,2:T(8,128)S(1)} %copy.145), channel_id=1, source_target_pairs={{0,4},{4,8},{8,12},{12,16},{16,20},{20,24},{24,28},{1,5},{5,9},{9,... | collective-permute-start | bytes 50696 | tf_op jit(solution)/shard_map/ppermute | solution.py:23
  212.7 6.2 %copy-start.14 = (f32[64,66,1]{2,1,0:T(8,128)S(1)}, f32[64,66,1]{2,1,0:T(8,128)}, u32[]{:S(2)}) copy-start(f32[64,66,1]{2,1,0:T(8,128)} %copy.147) | copy-start | bytes 50692
  301.5 6.7 %copy-start.5 = (f32[8,8,64,128]{3,2,1,0:T(8,128)}, f32[8,8,64,128]{3,2,1,0:T(8,128)S(1)}, u32[]{:S(2)}) copy-start(f32[8,8,64,128]{3,2,1,0:T(8,128)S(1)} %copy.172) | copy-start | bytes 6291460
  301.6 5.6 %collective-permute-start.9 = (f32[64,1,128]{2,0,1:T(8,128)S(1)}, f32[64,1,128]{2,0,1:T(8,128)S(1)}, u32[]{:S(2)}, u32[]{:S(2)}) collective-permute-start(f32[64,1,128]{2,0,1:T(8,128)S(1)} %bitcast.268), channel_id=1, source_target_pairs={{1,0},{2,1},{3,2},{32,3},{33,32},{34,33},{35,34},{64,35},{65,64},{... | collective-permute-start | bytes 98312 | tf_op jit(solution)/shard_map/ppermute | solution.py:25
  303.8 4.3 collective-permute-start.8
  313.8 9.3 %collective-permute-start.11 = (f32[64,66,1]{1,0,2:T(8,128)S(1)}, f32[64,66,1]{1,0,2:T(8,128)S(1)}, u32[]{:S(2)}, u32[]{:S(2)}) collective-permute-start(f32[64,66,1]{1,0,2:T(8,128)S(1)} %copy.158), channel_id=1, source_target_pairs={{4,0},{8,4},{12,8},{16,12},{20,16},{24,20},{28,24},{5,1},{9,5},{13... | collective-permute-start | bytes 50696 | tf_op jit(solution)/shard_map/ppermute | solution.py:25
  317.6 7.8 %collective-permute-start.10 = (f32[64,66,1]{1,0,2:T(8,128)S(1)}, f32[64,66,1]{1,0,2:T(8,128)S(1)}, u32[]{:S(2)}, u32[]{:S(2)}) collective-permute-start(f32[64,66,1]{1,0,2:T(8,128)S(1)} %copy.157), channel_id=1, source_target_pairs={{0,4},{4,8},{8,12},{12,16},{16,20},{20,24},{24,28},{1,5},{5,9},{9,... | collective-permute-start | bytes 50696 | tf_op jit(solution)/shard_map/ppermute | solution.py:23
  327.6 6.4 %copy-start.6 = (f32[8,8,64,128]{3,2,1,0:T(8,128)S(1)}, f32[8,8,64,128]{3,2,1,0:T(8,128)}, u32[]{:S(2)}) copy-start(f32[8,8,64,128]{3,2,1,0:T(8,128)} %copy-done.5) | copy-start | bytes 6291460
  327.6 6.4 %copy-start.9 = (f32[16,4,64,128]{3,2,0,1:T(8,128)S(1)}, f32[16,4,64,128]{3,2,0,1:T(8,128)}, u32[]{:S(2)}) copy-start(f32[16,4,64,128]{3,2,0,1:T(8,128)} %copy.128) | copy-start | bytes 6291460
  327.6 6.4 %copy-start.10 = (f32[64,66,1]{2,1,0:T(8,128)S(1)}, f32[64,66,1]{2,1,0:T(8,128)}, u32[]{:S(2)}) copy-start(f32[64,66,1]{2,1,0:T(8,128)} %copy.160) | copy-start | bytes 50692
  327.6 6.4 %copy-start.13 = (f32[64,66,1]{2,1,0:T(8,128)S(1)}, f32[64,66,1]{2,1,0:T(8,128)}, u32[]{:S(2)}) copy-start(f32[64,66,1]{2,1,0:T(8,128)} %copy.159) | copy-start | bytes 50692
  (9 other events, 45.0 us)
where the time goes:
time: 446 us; the launch traced here: 442 us
  blocking collectives  172 us (39%)
  matrix products  81.1 us (18%)
  other arithmetic  56.9 us (13%)
  local copies, waits for them, and re-layouts  52.2 us (12%)
  starting transfers between devices  47.2 us (11%)
  waiting for transfers between devices  21.8 us (5%)
  between operations  10.9 us (2%)
    psum x15, blocking collectives, over_axes(): x = lax.psum(x, axis)  122 us
    dot_general x24, matrix products, apply_blocks(): jnp.dot(matrices[member], flattened, precision=lax.Precision.HIGHEST)  81.1 us
    all_to_all x1, blocking collectives, sent_together(): lax.all_to_all(both, axis, split_axis=split_dim, concat_axis=concat_dim,...  50 us
    ppermute x6, starting transfers between devices, extended(): lax.ppermute(tail, axis, [(i, (i + 1) % count) for i in range(ends)])  26 us
    all_to_all x1, waiting for transfers between devices, per_device(): lax.all_to_all(right_side, GZ, split_axis=1, concat_axis=0, tiled=True)  19.8 us
    concatenate x6, other arithmetic, extended(): jnp.concatenate([lax.ppermute(tail, axis, [(i, (i + 1) % count) for i in...  19.1 us
    reduce_sum x3, other arithmetic, paired(): jnp.sum(image * precond)  17.7 us
    slice x6, local copies, waits for them, and re-layouts, extended(): head = lax.slice_in_dim(cells, 0, width, axis=dim)  15.9 us
  transfers between devices with their start and end apart: 14, of which 3 were waited for; matrix products, arithmetic and copies ran while one was open for 12% of the time, Pallas kernels for 0%

commit v1 on v0

--- a/solution.py
+++ b/solution.py
@@ -31,7 +31,8 @@
 
 def over_axes(x, axes):
     for axis in axes:
-        x = lax.psum(x, axis)
+        terms = lax.all_gather(x, axis)
+        x = jnp.sum(terms, axis=0)
     return x
 
 

time: 446 us -> 496 us (1.11)
  local copies, waits for them, and re-layouts: 52.2 us -> 96.6 us
  blocking collectives: 172 us -> 152 us
  other arithmetic: 56.9 us -> 76.2 us
  waiting for transfers between devices: 21.8 us -> 30.7 us
    psum x15 -> x0, blocking collectives: 122 us -> none  [over_axes(): x = lax.psum(x, axis)]
    unnamed x0 -> x15, blocking collectives: none -> 102 us
    unnamed x43 -> x118, local copies, waits for them, and re-layouts: 9.73 us -> 54.1 us
    reduce_sum x0 -> x30, other arithmetic: none -> 19.5 us  [over_axes(): x = jnp.sum(terms, axis=0)]
    ppermute x6, waiting for transfers between devices: 0.02 us -> 11.5 us  [extended(): lax.ppermute(head, axis, [((i + 1) % count, i) for i in range(ends)])]
  transfers between devices with their start and end apart: 14 -> 14, of which waited for: 3 -> 6; matrix products, arithmetic and copies ran while one was open for 12% -> 11% of each run, Pallas kernels for 0% -> 0%
where the time goes in v1:
time: 496 us; the launch traced here: 491 us
  blocking collectives  152 us (31%)
  local copies, waits for them, and re-layouts  96.6 us (19%)
  matrix products  81.5 us (16%)
  other arithmetic  76.2 us (15%)
  starting transfers between devices  42.9 us (9%)
  waiting for transfers between devices  30.7 us (6%)
  between operations  11.4 us (2%)
    unnamed x15, blocking collectives  102 us
    dot_general x24, matrix products, apply_blocks(): jnp.dot(matrices[member], flattened, precision=lax.Precision.HIGHEST)  81.5 us
    unnamed x118, local copies, waits for them, and re-layouts  54.1 us
    all_to_all x1, blocking collectives, sent_together(): lax.all_to_all(both, axis, split_axis=split_dim, concat_axis=concat_dim,...  50 us
    ppermute x6, starting transfers between devices, extended(): lax.ppermute(tail, axis, [(i, (i + 1) % count) for i in range(ends)])  22.3 us
    reduce_sum x30, other arithmetic, over_axes(): x = jnp.sum(terms, axis=0)  19.5 us
    all_to_all x1, waiting for transfers between devices, per_device(): lax.all_to_all(right_side, GZ, split_axis=1, concat_axis=0, tiled=True)  19.1 us
    concatenate x6, other arithmetic, extended(): jnp.concatenate([lax.ppermute(tail, axis, [(i, (i + 1) % count) for i in...  19 us
  transfers between devices with their start and end apart: 14, of which 6 were waited for; matrix products, arithmetic and copies ran while one was open for 11% of the time, Pallas kernels for 0%

profile of v1, /device:TPU:1, one launch (start us, length us, event | category | flops | bytes accessed | tf_op | source)
XLA Modules:
  0.0 491.0 jit_solution(13610078496204365989)
XLA Ops:
  4.8 5.0 %all-to-all-start = ((f32[16,256,128]{2,0,1:T(8,128)}), f32[16,256,128]{2,0,1:T(8,128)S(1)}, u32[]{:S(2)}, u32[]{:S(2)}) async-start(f32[16,256,128]{2,0,1:T(8,128)} %copy.125), calls=%async_computation | async-start | bytes 4194304 | tf_op jit(solution)/shard_map/all_to_all | solution.py:93
  15.3 19.1 %all-to-all-done = f32[16,256,128]{2,0,1:T(8,128)S(1)} async-done(((f32[16,256,128]{2,0,1:T(8,128)}), f32[16,256,128]{2,0,1:T(8,128)S(1)}, u32[]{:S(2)}, u32[]{:S(2)}) %all-to-all-start) | async-done | bytes 2097184 | tf_op jit(solution)/shard_map/all_to_all | solution.py:93
  34.4 5.5 %all-to-all-start.1 = ((f32[16,256,128]{2,0,1:T(8,128)}), f32[16,256,128]{2,0,1:T(8,128)}, u32[]{:S(2)}, u32[]{:S(2)}) async-start(f32[16,256,128]{2,0,1:T(8,128)} %copy.127), calls=%async_computation.1 | async-start | bytes 4194304 | tf_op jit(solution)/shard_map/all_to_all | solution.py:94
  101.4 5.4 %select_maximum_fusion.8 = f32[66,66,130]{2,1,0:T(8,128)S(1)} fusion(f32[64,66,1]{2,1,0:T(8,128)} %copy.136, f32[64,66,1]{2,1,0:T(8,128)} %copy.135, f32[64,1,128]{2,1,0:T(1,128)S(1)} %bitcast.284, f32[64,64,128]{2,1,0:T(8,128)S(1)} %bitcast.265, f32[64,1,128]{2,1,0:T(1,128)S(1)} %bitcast.281), kind=kLoop, calls=%fused_computation.55 | loop fusion | flops 6795360 | bytes 4461600 | tf_op jit(solution)/shard_map/concatenate | solution.py:21
  106.9 5.7 %multiply_reduce_fusion.4 = (f32[]{:T(128)}, f32[64,64,128]{2,1,0:T(8,128)}) fusion(f32[8,8,64,128]{3,2,1,0:T(8,128)S(1)} %copy.167, f32[64,1,128]{2,1,0:T(1,128)S(1)} %bitcast.285, f32[64,64,128]{2,1,0:T(8,128)S(1)} %bitcast.266, f32[64,1,128]{2,1,0:T(1,128)S(1)} %bitcast.282, f32[64,66,1]{2,1,0:T(8,128)S(1)} %copy-done.12, ...), kind=kLoop, calls=%fused_computation.144 | loop fusion | flops 8912895 | bytes 12682244 | tf_op jit(solution)/shard_map/reduce_sum | solution.py:87
  114.5 8.7 %all-reduce.38 = (f32[4]{0:T(128)S(1)}, f32[4]{0:T(128)S(1)}) all-reduce(f32[4]{0:T(128)S(1)} %dynamic-update-slice, f32[4]{0:T(128)S(1)} %dynamic-update-slice.5), channel_id=1, replica_groups=mesh['gx'=4,'gy_0'=4,'gy_1'=2,'gz_0'=2,'gz_1'=2] {'gx'}, use_global_device_ids=true, to_apply=%add.3 | all-reduce | flops 8 | bytes 64
  127.7 11.5 %all-reduce.35 = (f32[4]{0:T(128)S(1)}, f32[4]{0:T(128)S(1)}) all-reduce(f32[4]{0:T(128)S(1)} %dynamic-update-slice.1, f32[4]{0:T(128)S(1)} %dynamic-update-slice.6), channel_id=1, replica_groups=mesh['gx'=4,'gy_0'=4,'gy_1'=2,'gz_0'=2,'gz_1'=2] {'gy_0'}, use_global_device_ids=true, to_apply=%add.4 | all-reduce | flops 8 | bytes 64
  143.8 5.3 %all-reduce.47 = (f32[2]{0:T(128)S(1)}, f32[2]{0:T(128)S(1)}) all-reduce(f32[2]{0:T(128)S(1)} %dynamic-update-slice.2, f32[2]{0:T(128)S(1)} %dynamic-update-slice.7), channel_id=1, replica_groups=mesh['gx'=4,'gy_0'=4,'gy_1'=2,'gz_0'=2,'gz_1'=2] {'gy_1'}, use_global_device_ids=true, to_apply=%add.5 | all-reduce | flops 4 | bytes 32
  161.6 10.0 %all-reduce.41 = (f32[2]{0:T(128)S(1)}, f32[2]{0:T(128)S(1)}) all-reduce(f32[2]{0:T(128)S(1)} %dynamic-update-slice.4, f32[2]{0:T(128)S(1)} %dynamic-update-slice.9), channel_id=1, replica_groups=mesh['gx'=4,'gy_0'=4,'gy_1'=2,'gz_0'=2,'gz_1'=2] {'gz_1'}, use_global_device_ids=true, to_apply=%add.7 | all-reduce | flops 4 | bytes 32
  233.8 6.2 %select_maximum_fusion.4 = f32[66,66,130]{2,1,0:T(8,128)S(1)} fusion(f32[64,66,1]{2,1,0:T(8,128)} %copy.148, f32[64,66,1]{2,1,0:T(8,128)} %copy.147, f32[64,1,128]{2,1,0:T(1,128)S(1)} %bitcast.296, f32[64,64,128]{2,1,0:T(8,128)} %bitcast.269, f32[64,1,128]{2,1,0:T(1,128)S(1)} %bitcast.290), kind=kLoop, calls=%fused_computation.51 | loop fusion | flops 6795360 | bytes 4461600 | tf_op jit(solution)/shard_map/concatenate | solution.py:21
  240.1 6.0 %multiply_reduce_fusion.2 = (f32[]{:T(128)}, f32[]{:T(128)}, f32[64,64,128]{2,1,0:T(8,128)}) fusion(f32[8,8,64,128]{3,2,1,0:T(8,128)S(1)} %copy-done.4, f32[64,64,128]{2,1,0:T(8,128)S(1)} %bitcast_subtract_fusion, f32[64,1,128]{2,1,0:T(1,128)S(1)} %bitcast.297, f32[64,64,128]{2,1,0:T(8,128)S(1)} %bitcast.270, f32[64,1,128]{2,1,0:T(1,128)S(1)} %bitcast.291, ...), kind=kLoop, calls=%fused_computation.142 | loop fusion | flops 9961470 | bytes 14779400 | tf_op jit(solution)/shard_map/reduce_sum | solution.py:87
  248.9 6.0 %all-reduce.37 = (f32[4]{0:T(128)S(1)}, f32[4]{0:T(128)S(1)}) all-reduce(f32[4]{0:T(128)S(1)} %dynamic-update-slice.10, f32[4]{0:T(128)S(1)} %dynamic-update-slice.15), channel_id=1, replica_groups=mesh['gx'=4,'gy_0'=4,'gy_1'=2,'gz_0'=2,'gz_1'=2] {'gx'}, use_global_device_ids=true, to_apply=%add.13 | all-reduce | flops 8 | bytes 64
  258.8 6.0 %all-reduce.34 = (f32[4]{0:T(128)S(1)}, f32[4]{0:T(128)S(1)}) all-reduce(f32[4]{0:T(128)S(1)} %dynamic-update-slice.11, f32[4]{0:T(128)S(1)} %dynamic-update-slice.16), channel_id=1, replica_groups=mesh['gx'=4,'gy_0'=4,'gy_1'=2,'gz_0'=2,'gz_1'=2] {'gy_0'}, use_global_device_ids=true, to_apply=%add.14 | all-reduce | flops 8 | bytes 64
  268.8 5.3 %all-reduce.46 = (f32[2]{0:T(128)S(1)}, f32[2]{0:T(128)S(1)}) all-reduce(f32[2]{0:T(128)S(1)} %dynamic-update-slice.12, f32[2]{0:T(128)S(1)} %dynamic-update-slice.17), channel_id=1, replica_groups=mesh['gx'=4,'gy_0'=4,'gy_1'=2,'gz_0'=2,'gz_1'=2] {'gy_1'}, use_global_device_ids=true, to_apply=%add.15 | all-reduce | flops 4 | bytes 32
  286.3 9.3 %all-reduce.40 = (f32[2]{0:T(128)S(1)}, f32[2]{0:T(128)S(1)}) all-reduce(f32[2]{0:T(128)S(1)} %dynamic-update-slice.14, f32[2]{0:T(128)S(1)} %dynamic-update-slice.19), channel_id=1, replica_groups=mesh['gx'=4,'gy_0'=4,'gy_1'=2,'gz_0'=2,'gz_1'=2] {'gz_1'}, use_global_device_ids=true, to_apply=%add.17 | all-reduce | flops 4 | bytes 32
  346.1 5.4 %collective-permute-start.10 = (f32[64,66,1]{1,0,2:T(8,128)S(1)}, f32[64,66,1]{1,0,2:T(8,128)S(1)}, u32[]{:S(2)}, u32[]{:S(2)}) collective-permute-start(f32[64,66,1]{1,0,2:T(8,128)S(1)} %copy.157), channel_id=1, source_target_pairs={{0,4},{4,8},{8,12},{12,16},{16,20},{20,24},{24,28},{1,5},{5,9},{9,... | collective-permute-start | bytes 50696 | tf_op jit(solution)/shard_map/ppermute | solution.py:23
  362.3 6.2 %select_maximum_fusion = f32[66,66,130]{2,1,0:T(8,128)S(1)} fusion(f32[64,66,1]{2,1,0:T(8,128)} %copy.160, f32[64,66,1]{2,1,0:T(8,128)} %copy.159, f32[64,1,128]{2,1,0:T(1,128)S(1)} %bitcast.293, f32[64,64,128]{2,1,0:T(8,128)} %bitcast.273, f32[64,1,128]{2,1,0:T(1,128)S(1)} %bitcast.287), kind=kLoop, calls=%fused_computation.47 | loop fusion | flops 6795360 | bytes 4461600 | tf_op jit(solution)/shard_map/concatenate | solution.py:21
  368.6 6.0 %multiply_reduce_fusion = (f32[]{:T(128)}, f32[]{:T(128)}, f32[64,64,128]{2,1,0:T(8,128)}) fusion(f32[8,8,64,128]{3,2,1,0:T(8,128)S(1)} %copy-done.6, f32[64,64,128]{2,1,0:T(8,128)S(1)} %multiply_subtract_fusion.1, f32[64,1,128]{2,1,0:T(1,128)S(1)} %bitcast.294, f32[64,64,128]{2,1,0:T(8,128)S(1)} %bitcast.274, f32[64,1,128]{2,1,0:T(1,128)S(1)} %bitcast.288, ...), kind=kLoop, calls=%fused_computation.138 | loop fusion | flops 9961470 | bytes 14779400 | tf_op jit(solution)/shard_map/reduce_sum | solution.py:87
  377.3 8.3 %all-reduce.36 = (f32[4]{0:T(128)S(1)}, f32[4]{0:T(128)S(1)}) all-reduce(f32[4]{0:T(128)S(1)} %dynamic-update-slice.20, f32[4]{0:T(128)S(1)} %dynamic-update-slice.25), channel_id=1, replica_groups=mesh['gx'=4,'gy_0'=4,'gy_1'=2,'gz_0'=2,'gz_1'=2] {'gx'}, use_global_device_ids=true, to_apply=%add.23 | all-reduce | flops 8 | bytes 64
  389.5 6.1 %all-reduce.33 = (f32[4]{0:T(128)S(1)}, f32[4]{0:T(128)S(1)}) all-reduce(f32[4]{0:T(128)S(1)} %dynamic-update-slice.21, f32[4]{0:T(128)S(1)} %dynamic-update-slice.26), channel_id=1, replica_groups=mesh['gx'=4,'gy_0'=4,'gy_1'=2,'gz_0'=2,'gz_1'=2] {'gy_0'}, use_global_device_ids=true, to_apply=%add.24 | all-reduce | flops 8 | bytes 64
  399.5 5.3 %all-reduce.45 = (f32[2]{0:T(128)S(1)}, f32[2]{0:T(128)S(1)}) all-reduce(f32[2]{0:T(128)S(1)} %dynamic-update-slice.22, f32[2]{0:T(128)S(1)} %dynamic-update-slice.27), channel_id=1, replica_groups=mesh['gx'=4,'gy_0'=4,'gy_1'=2,'gz_0'=2,'gz_1'=2] {'gy_1'}, use_global_device_ids=true, to_apply=%add.25 | all-reduce | flops 4 | bytes 32
  416.8 8.8 %all-reduce.39 = (f32[2]{0:T(128)S(1)}, f32[2]{0:T(128)S(1)}) all-reduce(f32[2]{0:T(128)S(1)} %dynamic-update-slice.24, f32[2]{0:T(128)S(1)} %dynamic-update-slice.29), channel_id=1, replica_groups=mesh['gx'=4,'gy_0'=4,'gy_1'=2,'gz_0'=2,'gz_1'=2] {'gz_1'}, use_global_device_ids=true, to_apply=%add.27 | all-reduce | flops 4 | bytes 32
  430.8 6.5 %multiply_subtract_fusion = (f32[64,64,128]{2,1,0:T(8,128)S(1)}, f32[64,64,128]{2,1,0:T(8,128)S(1)}) fusion(f32[64,64,128]{2,1,0:T(8,128)S(1)} %multiply_subtract_fusion.1, f32[64,64,128]{2,1,0:T(8,128)} %get-tuple-element.36, f32[]{:T(128)S(6)} %div.25, f32[]{:T(128)S(6)} %div.27, f32[64,64,128]{2,1,0:T(8,128)} %get-tuple-element.37, ...), kind=kLoop, calls=%fused_computation.136 | loop fusion | flops 7864320 | bytes 18874388 | tf_op jit(solution)/shard_map/sub | solution.py:106
  437.7 50.0 %all_to_all.45 = f32[64,64,256]{2,1,0:T(8,128)S(1)} all-to-all(f32[64,64,256]{2,1,0:T(8,128)S(1)} %pad_maximum_fusion), channel_id=1, replica_groups=mesh['gx'=4,'gy_0'=4,'gy_1'=2,'gz_0'=2,'gz_1'=2] {'gz_0','gz_1'}, dimensions={0} | all-to-all | bytes 8388608 | tf_op jit(solution)/shard_map/all_to_all | solution.py:47
  (230 shorter events, 262.1 us)
Async XLA Ops:
  4.8 29.7 %all-to-all-start = ((f32[16,256,128]{2,0,1:T(8,128)}), f32[16,256,128]{2,0,1:T(8,128)S(1)}, u32[]{:S(2)}, u32[]{:S(2)}) async-start(f32[16,256,128]{2,0,1:T(8,128)} %copy.125), calls=%async_computation | async-start | bytes 4194304 | tf_op jit(solution)/shard_map/all_to_all | solution.py:93
  34.4 38.5 %all-to-all-start.1 = ((f32[16,256,128]{2,0,1:T(8,128)}), f32[16,256,128]{2,0,1:T(8,128)}, u32[]{:S(2)}, u32[]{:S(2)}) async-start(f32[16,256,128]{2,0,1:T(8,128)} %copy.127), calls=%async_computation.1 | async-start | bytes 4194304 | tf_op jit(solution)/shard_map/all_to_all | solution.py:94
  40.6 22.8 %copy-start.1 = (f32[16,4,64,128]{3,2,0,1:T(8,128)}, f32[16,4,64,128]{3,2,0,1:T(8,128)S(1)}, u32[]{:S(2)}) copy-start(f32[16,4,64,128]{3,2,0,1:T(8,128)S(1)} %copy.126) | copy-start | bytes 6291460
  67.4 39.4 %copy-start.2 = (f32[8,8,64,128]{3,2,1,0:T(8,128)}, f32[8,8,64,128]{3,2,1,0:T(8,128)S(1)}, u32[]{:S(2)}) copy-start(f32[8,8,64,128]{3,2,1,0:T(8,128)S(1)} %copy.167) | copy-start | bytes 6291460
  67.4 8.5 %collective-permute-start = (f32[64,1,128]{2,0,1:T(8,128)S(1)}, f32[64,1,128]{2,0,1:T(8,128)S(1)}, u32[]{:S(2)}, u32[]{:S(2)}) collective-permute-start(f32[64,1,128]{2,0,1:T(8,128)S(1)} %bitcast.299), channel_id=1, source_target_pairs={{0,1},{1,2},{2,3},{3,32},{32,33},{33,34},{34,35},{35,64},{64,65},{... | collective-permute-start | bytes 98312 | tf_op jit(solution)/shard_map/ppermute | solution.py:23
  71.0 5.2 %collective-permute-start.1 = (f32[64,1,128]{2,0,1:T(8,128)S(1)}, f32[64,1,128]{2,0,1:T(8,128)S(1)}, u32[]{:S(2)}, u32[]{:S(2)}) collective-permute-start(f32[64,1,128]{2,0,1:T(8,128)S(1)} %bitcast.298), channel_id=1, source_target_pairs={{1,0},{2,1},{3,2},{32,3},{33,32},{34,33},{35,34},{64,35},{65,64},{... | collective-permute-start | bytes 98312 | tf_op jit(solution)/shard_map/ppermute | solution.py:25
  81.9 15.0 %collective-permute-start.2 = (f32[64,66,1]{1,0,2:T(8,128)S(1)}, f32[64,66,1]{1,0,2:T(8,128)S(1)}, u32[]{:S(2)}, u32[]{:S(2)}) collective-permute-start(f32[64,66,1]{1,0,2:T(8,128)S(1)} %copy.133), channel_id=1, source_target_pairs={{0,4},{4,8},{8,12},{12,16},{16,20},{20,24},{24,28},{1,5},{5,9},{9,... | collective-permute-start | bytes 50696 | tf_op jit(solution)/shard_map/ppermute | solution.py:23
  89.1 10.0 %collective-permute-start.3 = (f32[64,66,1]{1,0,2:T(8,128)S(1)}, f32[64,66,1]{1,0,2:T(8,128)S(1)}, u32[]{:S(2)}, u32[]{:S(2)}) collective-permute-start(f32[64,66,1]{1,0,2:T(8,128)S(1)} %copy.134), channel_id=1, source_target_pairs={{4,0},{8,4},{12,8},{16,12},{20,16},{24,20},{28,24},{5,1},{9,5},{13... | collective-permute-start | bytes 50696 | tf_op jit(solution)/shard_map/ppermute | solution.py:25
  106.8 7.1 %copy-start.22 = (u32[128]{0:T(128)S(1)}, u32[128]{0:T(128)}, u32[]{:S(2)}) copy-start(u32[128]{0:T(128)} %constant.47) | copy-start | bytes 1540
  106.9 20.3 %copy-start.21 = (u32[128]{0:T(128)S(1)}, u32[128]{0:T(128)}, u32[]{:S(2)}) copy-start(u32[128]{0:T(128)} %constant.52) | copy-start | bytes 1540
  106.9 36.3 %copy-start.20 = (u32[128]{0:T(128)S(1)}, u32[128]{0:T(128)}, u32[]{:S(2)}) copy-start(u32[128]{0:T(128)} %constant.57) | copy-start | bytes 1540
  106.9 46.2 %copy-start.19 = (u32[128]{0:T(128)S(1)}, u32[128]{0:T(128)}, u32[]{:S(2)}) copy-start(u32[128]{0:T(128)} %constant.62) | copy-start | bytes 1540
  177.0 63.1 %copy-start = (f32[64,64,128]{2,1,0:T(8,128)}, f32[64,64,128]{2,1,0:T(8,128)S(1)}, u32[]{:S(2)}) copy-start(f32[64,64,128]{2,1,0:T(8,128)S(1)} %bitcast_subtract_fusion) | copy-start | bytes 6291460
  205.3 8.2 %copy-start.3 = (f32[8,8,64,128]{3,2,1,0:T(8,128)}, f32[8,8,64,128]{3,2,1,0:T(8,128)S(1)}, u32[]{:S(2)}) copy-start(f32[8,8,64,128]{3,2,1,0:T(8,128)S(1)} %copy.170) | copy-start | bytes 6291460
  205.3 4.9 collective-permute-start.4
  208.3 5.2 %collective-permute-start.5 = (f32[64,1,128]{2,0,1:T(8,128)S(1)}, f32[64,1,128]{2,0,1:T(8,128)S(1)}, u32[]{:S(2)}, u32[]{:S(2)}) collective-permute-start(f32[64,1,128]{2,0,1:T(8,128)S(1)} %bitcast.300), channel_id=1, source_target_pairs={{1,0},{2,1},{3,2},{32,3},{33,32},{34,33},{35,34},{64,35},{65,64},{... | collective-permute-start | bytes 98312 | tf_op jit(solution)/shard_map/ppermute | solution.py:25
  219.2 7.5 %collective-permute-start.6 = (f32[64,66,1]{1,0,2:T(8,128)S(1)}, f32[64,66,1]{1,0,2:T(8,128)S(1)}, u32[]{:S(2)}, u32[]{:S(2)}) collective-permute-start(f32[64,66,1]{1,0,2:T(8,128)S(1)} %copy.145), channel_id=1, source_target_pairs={{0,4},{4,8},{8,12},{12,16},{16,20},{20,24},{24,28},{1,5},{5,9},{9,... | collective-permute-start | bytes 50696 | tf_op jit(solution)/shard_map/ppermute | solution.py:23
  225.4 6.2 %collective-permute-start.7 = (f32[64,66,1]{1,0,2:T(8,128)S(1)}, f32[64,66,1]{1,0,2:T(8,128)S(1)}, u32[]{:S(2)}, u32[]{:S(2)}) collective-permute-start(f32[64,66,1]{1,0,2:T(8,128)S(1)} %copy.146), channel_id=1, source_target_pairs={{4,0},{8,4},{12,8},{16,12},{20,16},{24,20},{28,24},{5,1},{9,5},{13... | collective-permute-start | bytes 50696 | tf_op jit(solution)/shard_map/ppermute | solution.py:25
  333.2 7.2 %copy-start.5 = (f32[8,8,64,128]{3,2,1,0:T(8,128)}, f32[8,8,64,128]{3,2,1,0:T(8,128)S(1)}, u32[]{:S(2)}) copy-start(f32[8,8,64,128]{3,2,1,0:T(8,128)S(1)} %copy.172) | copy-start | bytes 6291460
  333.2 4.3 collective-permute-start.8
  335.2 5.2 %collective-permute-start.9 = (f32[64,1,128]{2,0,1:T(8,128)S(1)}, f32[64,1,128]{2,0,1:T(8,128)S(1)}, u32[]{:S(2)}, u32[]{:S(2)}) collective-permute-start(f32[64,1,128]{2,0,1:T(8,128)S(1)} %bitcast.301), channel_id=1, source_target_pairs={{1,0},{2,1},{3,2},{32,3},{33,32},{34,33},{35,34},{64,35},{65,64},{... | collective-permute-start | bytes 98312 | tf_op jit(solution)/shard_map/ppermute | solution.py:25
  346.1 9.1 %collective-permute-start.10 = (f32[64,66,1]{1,0,2:T(8,128)S(1)}, f32[64,66,1]{1,0,2:T(8,128)S(1)}, u32[]{:S(2)}, u32[]{:S(2)}) collective-permute-start(f32[64,66,1]{1,0,2:T(8,128)S(1)} %copy.157), channel_id=1, source_target_pairs={{0,4},{4,8},{8,12},{12,16},{16,20},{20,24},{24,28},{1,5},{5,9},{9,... | collective-permute-start | bytes 50696 | tf_op jit(solution)/shard_map/ppermute | solution.py:23
  353.9 6.2 %collective-permute-start.11 = (f32[64,66,1]{1,0,2:T(8,128)S(1)}, f32[64,66,1]{1,0,2:T(8,128)S(1)}, u32[]{:S(2)}, u32[]{:S(2)}) collective-permute-start(f32[64,66,1]{1,0,2:T(8,128)S(1)} %copy.158), channel_id=1, source_target_pairs={{4,0},{8,4},{12,8},{16,12},{20,16},{24,20},{28,24},{5,1},{9,5},{13... | collective-permute-start | bytes 50696 | tf_op jit(solution)/shard_map/ppermute | solution.py:25
  362.3 6.3 %copy-start.13 = (f32[64,66,1]{2,1,0:T(8,128)S(1)}, f32[64,66,1]{2,1,0:T(8,128)}, u32[]{:S(2)}) copy-start(f32[64,66,1]{2,1,0:T(8,128)} %copy.160) | copy-start | bytes 50692
  (14 other events, 74.0 us)
